TPU v7x, 32 devices: a whole 2x2x4 slice. The times are simulated.
32 devices in a mesh: dp: 2 (over core), expert: 4 (over y, x), mp: 4 (over z).
Axes of the slice: x: 2, y: 2, z: 4, core: 2. Of those that a mesh axis runs over, the one named last changes fastest.
Arguments:
- hidden: bfloat16 [3072, 2, 7168], P(('dp', 'expert'), None, 'mp'), may hold values from -6 to 6
- cotangent: bfloat16 [3072, 2048], P(('dp', 'expert'), 'mp'), may hold values from -6 to 6
- routes: int32 [3072, 2], P(('dp', 'expert')), may hold values from 0 to 3, all different within a row; in each aligned block of 384 rows (0 to 383, 384 to 767, ...) at most 288 rows name the same one
- combine: float32 [3072, 2], P(('dp', 'expert')), may hold values from 0.1 to 0.9
- block_pair: int32 [8, 12], P(('dp', 'expert')), may hold values from 0 to 11, each once within a row
- lengths: int32 [8, 12], P(('dp', 'expert')), may hold values from 4 to 32
- log_ratio: float32 [8, 12], P(('dp', 'expert')), may hold values from -30 to 30
Outputs:
- grad_down: float32 [4, 7168, 2048], P('expert', ('mp', 'dp'))
- expert_load: float32 [4], replicated
Inputs may be any that keep to these rules, and one draw needn't show every extreme that they name: `routes`: each row names 2 different experts; in each aligned block of 384 rows (the rows of one device) no expert is named more than 288 times, and in some blocks one expert is named exactly 288 times. `block_pair`: each row holds every number of 0 to 11 once; value v marks the chosen response of the row's pair v // 2 if v is even, its rejected response if v is odd.
All inputs are finite; a program needn't handle non-finite values.
Results may differ from a plain program's by a relative error of at most 0.0029.
Values may be sent and summed in bfloat16 or wider, within the bound.
No kernel may reach another device: no remote copies, remote signals or barrier semaphores. Data moves between devices by JAX's collectives and lax.ppermute only.
A program may use at most 128 MiB of HBM per device.

v0:
```python
import jax
import jax.numpy as jnp
from jax import lax
from jax.sharding import PartitionSpec as P

EXP_DEV = 1
LEN = 32
beta_scale = 0.1


def token_weights(combine, block_pair, lengths, log_ratio, block_len):
    blocks = block_pair.shape[1]
    labels = jnp.arange(blocks, dtype=jnp.int32)
    matches = block_pair[:, :, None] == labels[None, None, :]
    by_label = jnp.sum(jnp.where(matches, log_ratio[:, :, None], 0.0), axis=1)
    margin = by_label[:, 0::2] - by_label[:, 1::2]
    pair_coef = beta_scale * jax.nn.sigmoid(-beta_scale * margin)
    owners = block_pair // 2
    pair_ids = jnp.arange(blocks // 2, dtype=jnp.int32)
    picked = owners[:, :, None] == pair_ids[None, None, :]
    block_coef = jnp.sum(jnp.where(picked, pair_coef[:, None, :], 0.0), axis=2)
    block_weight = jnp.where(block_pair % 2 == 0, -block_coef, block_coef)
    position = jnp.arange(block_len, dtype=jnp.int32)
    within = position[None, None, :] < lengths[:, :, None]
    per_token = jnp.where(within, block_weight[:, :, None], 0.0).reshape(-1)
    return (combine * per_token[:, None], within.reshape(-1))


def body(hidden, cotangent, routes, combine, block_pair, lengths, log_ratio):
    weight, within = token_weights(combine, block_pair, lengths, log_ratio, LEN)
    tok_rows = routes.shape[0]
    route_top = routes.shape[1]
    ff_local = hidden.shape[2]
    groups = lax.axis_size("expert")
    experts = groups * EXP_DEV
    most_rows = 3 * tok_rows // 4
    labels = jnp.arange(experts, dtype=jnp.int32)
    routed = routes[:, :, None] == labels[None, None, :]
    local_load = jnp.sum(jnp.where(routed & within[:, None, None], 1.0, 0.0), axis=(0, 1)).astype(
        jnp.float32
    )
    flat_rows = tok_rows * route_top
    flat_hits = routed.reshape(flat_rows, experts).astype(jnp.int32)
    rank_of = jnp.sum((jnp.cumsum(flat_hits, axis=0) - 1) * flat_hits, axis=1)
    slot_of = routes.reshape(flat_rows) * most_rows + rank_of
    source = (
        jnp.zeros((experts * most_rows,), jnp.int32)
        .at[slot_of]
        .set(jnp.arange(flat_rows, dtype=jnp.int32))
    )
    filled = jnp.zeros((experts * most_rows,), jnp.float32).at[slot_of].set(1.0)
    token_of = source // route_top
    slot_weight = jnp.take(weight.reshape(flat_rows), source) * filled
    packed_h = jnp.take(hidden.reshape(flat_rows, ff_local), source, axis=0).reshape(
        groups, EXP_DEV * most_rows, ff_local
    )
    narrow_s = (
        slot_weight[:, None] * jnp.take(cotangent, token_of, axis=0).astype(jnp.float32)
    ).astype(jnp.bfloat16)
    moved_h, narrow = (
        lax.all_to_all(packed_h, "expert", split_axis=0, concat_axis=0, tiled=True),
        lax.all_to_all(
            narrow_s.reshape(groups, EXP_DEV * most_rows, cotangent.shape[1]),
            "expert",
            split_axis=0,
            concat_axis=0,
            tiled=True,
        ),
    )
    moved_s = lax.all_gather(narrow, "mp", axis=2, tiled=True)
    moved_h = moved_h.reshape(groups, EXP_DEV, most_rows, ff_local)
    moved_s = moved_s.reshape(groups, EXP_DEV, most_rows, moved_s.shape[2])
    products = [
        lax.dot_general(
            moved_h[:, 0],
            moved_s[:, 0],
            (((0, 1), (0, 1)), ((), ())),
            preferred_element_type=jnp.float32,
        )
    ]
    owned = lax.psum_scatter(jnp.stack(products, axis=1), "dp", scatter_dimension=0, tiled=True)
    grad_down = jnp.transpose(owned, (1, 0, 2))
    expert_load = lax.psum(local_load, ("dp", "expert"))
    return (grad_down, expert_load)


def solution(mesh):
    in_specs = (
        P(("dp", "expert"), None, "mp"),
        P(("dp", "expert"), "mp"),
        P(("dp", "expert"), None),
        P(("dp", "expert"), None),
        P(("dp", "expert"), None),
        P(("dp", "expert"), None),
        P(("dp", "expert"), None),
    )
    out_specs = (P("expert", ("mp", "dp"), None), P())
    return jax.shard_map(body, mesh=mesh, in_specs=in_specs, out_specs=out_specs, check_vma=False)
```

profile of v0, /device:TPU:0, one launch (start us, length us, event | category | flops | bytes accessed | tf_op | source)
XLA Modules:
  0.0 187.8 jit_solution(6503914561430639834)
XLA Ops:
  7.2 0.8 fusion.6
  8.2 0.7 fusion.14
  8.9 0.7 broadcast_multiply_fusion.1
  9.6 0.8 copy.16
  10.4 0.1 eq.83
  10.6 0.1 eq.79
  10.7 0.1 copy.15
  10.9 0.2 mul.49
  11.0 1.1 reduce-window.6
  12.2 0.2 slice_reduce_fusion
  12.4 0.2 reduce-window.9
  12.7 3.4 %scatter_custom_fusion = s32[1152]{0:T(1024)S(1)} fusion(s32[768]{0:T(1024)S(1)} %fusion.11, s32[768]{0:T(1024)S(1)} %iota.36, s32[]{:T(128)} %constant.86.clone.1), kind=kCustom, calls=%fused_computation.39 | custom fusion | bytes 4612 | tf_op jit(solution)/shard_map/scatter | solution.py:49
  16.3 0.7 fusion.13
  17.1 0.7 broadcast_reduce_fusion.1
  18.0 0.7 broadcast_multiply_fusion
  18.7 0.1 copy.18
  18.9 0.1 reshape.294
  19.0 3.4 %scatter_custom_fusion.1 = f32[1152]{0:T(1024)S(1)} fusion(s32[768]{0:T(1024)S(1)} %fusion.11, f32[768]{0:T(1024)S(1)} %broadcast.245, f32[]{:T(128)} %constant.96.clone.1), kind=kCustom, calls=%fused_computation.37 | custom fusion | bytes 4612 | tf_op jit(solution)/shard_map/scatter | solution.py:51
  22.4 4.6 %gather_fusion.1 = f32[1152]{0:T(1024)S(1)} fusion(f32[768]{0:T(1024)S(1)} %reshape.294, s32[2048]{0:T(1024)S(1)} %pad_clamp_fusion.1), kind=kCustom, calls=%fused_computation.1 | custom fusion | bytes 13824 | tf_op jit(solution)/shard_map/jit(_take)/gather | solution.py:53
  27.2 4.2 %gather_fusion.2 = bf16[1152,512]{1,0:T(8,128)(2,1)S(1)} fusion(bf16[384,512]{1,0:T(8,128)(2,1)S(1)} %copy-done, s32[2048]{0:T(1024)S(1)} %pad_clamp_fusion), kind=kCustom, calls=%fused_computation.2 | custom fusion | bytes 2363904 | tf_op jit(solution)/shard_map/jit(_take)/gather | solution.py:58
  31.5 0.4 multiply_convert_fusion
  31.8 20.6 %all_to_all.10 = bf16[4,288,512]{2,1,0:T(8,128)(2,1)} all-to-all(bf16[4,288,512]{2,1,0:T(8,128)(2,1)S(1)} %multiply_convert_fusion), channel_id=1, replica_groups=mesh['dp'=2,'expert'=4,'mp'=4] {'expert'}, dimensions={0} | all-to-all | bytes 2359296 | tf_op jit(solution)/shard_map/all_to_all | solution.py:62
  52.6 5.7 %reshape.293 = bf16[768,1792]{1,0:T(8,128)(2,1)S(1)} reshape(bf16[384,2,1792]{2,1,0:T(2,128)(2,1)} %param.7) | data formatting | bytes 5505024 | tf_op jit(solution)/shard_map/reshape | solution.py:54
  58.4 5.6 %gather_fusion = bf16[1152,1792]{1,0:T(8,128)(2,1)} fusion(bf16[768,1792]{1,0:T(8,128)(2,1)S(1)} %reshape.293, s32[2048]{0:T(1024)S(1)} %pad_clamp_fusion.1), kind=kCustom, calls=%fused_computation | custom fusion | bytes 8262144 | tf_op jit(solution)/shard_map/jit(_take)/gather | solution.py:54
  64.0 2.6 %broadcast_select_fusion = bf16[4,288,1792]{2,1,0:T(8,128)(2,1)S(1)} fusion(bf16[4,288,1792]{2,1,0:T(8,128)(2,1)} %bitcast.39, pred[4,288]{1,0:T(4,128)(4,1)S(1)} %broadcast_in_dim.106), kind=kLoop, calls=%fused_computation.6 | loop fusion | flops 2064384 | bytes 8258688 | tf_op jit(solution)/shard_map/jit(_take)/select_n | solution.py:54
  66.6 49.7 %all_to_all.11 = bf16[4,288,1792]{2,1,0:T(8,128)(2,1)} all-to-all(bf16[4,288,1792]{2,1,0:T(8,128)(2,1)S(1)} %broadcast_select_fusion), channel_id=1, replica_groups=mesh['dp'=2,'expert'=4,'mp'=4] {'expert'}, dimensions={0} | all-to-all | bytes 8257536 | tf_op jit(solution)/shard_map/all_to_all | solution.py:61
  116.4 25.4 %all-gather.2.cloned.1.call-done = bf16[4,288,2048]{2,1,0:T(8,128)(2,1)} async-done(((bf16[4,288,512]{2,1,0:T(8,128)(2,1)}), bf16[4,288,2048]{2,1,0:T(8,128)(2,1)}) %all-gather.2.cloned.1.call-update) | async-done | bytes 4718608 | tf_op jit(solution)/shard_map/all_gather | solution.py:70
  141.8 15.8 %convolution_bitcast_fusion = f32[1792,1,2048]{2,0,1:T(8,128)} fusion(bf16[4,288,1792]{2,1,0:T(8,128)(2,1)} %all_to_all.11, bf16[4,288,2048]{2,1,0:T(8,128)(2,1)} %all-gather.2.cloned.1.call-done), kind=kOutput, calls=%fused_computation.5 | convolution fusion | flops 8455716864 | bytes 23527424 | tf_op jit(solution)/shard_map/dot_general | solution.py:74
  157.6 0.7 copy-done.1
  158.2 0.1 select_reduce_fusion
  158.3 14.8 %psum.7 = f32[4]{0:T(128)} all-reduce(f32[4]{0:T(128)S(1)} %select_reduce_fusion), channel_id=1, replica_groups=mesh['dp'=2,'expert'=4,'mp'=4] {'dp','expert'}, use_global_device_ids=true, to_apply=%region_9.10 | all-reduce | flops 4 | bytes 32 | tf_op jit(solution)/shard_map/psum | solution.py:83
  173.1 7.8 %reduce-scatter.2.cloned.1.call-done = f32[896,1,2048]{2,0,1:T(8,128)} async-done(((f32[1792,1,2048]{2,0,1:T(8,128)}), f32[896,1,2048]{2,0,1:T(8,128)}) %reduce-scatter.2.cloned.1.call-update) | async-done | bytes 7340048 | tf_op jit(solution)/shard_map/reduce_scatter | solution.py:81
  (31 shorter events, 1.2 us)
Async XLA Ops:
  7.2 20.0 %copy-start = (bf16[384,512]{1,0:T(8,128)(2,1)S(1)}, bf16[384,512]{1,0:T(8,128)(2,1)}, u32[]{:S(2)}) copy-start(bf16[384,512]{1,0:T(8,128)(2,1)} %param.8) | copy-start | bytes 1179652
  7.2 134.6 %all-gather.2.cloned.1.call-start = ((), (), s32[]{:S(2)}) async-start(), calls=%async_computation.3 | async-start | bytes 5898240 | tf_op jit(solution)/shard_map/all_gather | solution.py:70
  52.5 128.4 %reduce-scatter.2.cloned.1.call-start = ((), (), s32[]{:S(2)}) async-start(), calls=%async_computation.4 | async-start | bytes 22020096 | tf_op jit(solution)/shard_map/reduce_scatter | solution.py:81
  157.5 0.7 copy-start.1
Sparse Core Ops, SparseCore 0:
  52.6 89.0 all-gather.1
  157.7 23.2 reduce-scatter.1
where the time goes:
time: 188 us
  blocking collectives  85.2 us (45%)
  waiting for transfers between devices  33.3 us (18%)
  local copies, waits for them, and re-layouts  31 us (16%)
  matrix products  15.8 us (8%)
  between operations  14.3 us (8%)
  other arithmetic  8.25 us (4%)
    all_to_all x1, blocking collectives, body(): lax.all_to_all(packed_h, 'expert', split_axis=0, concat_axis=0, tiled=True)  49.7 us
    all_gather x1, waiting for transfers between devices, body(): moved_s = lax.all_gather(narrow, 'mp', axis=2, tiled=True)  25.4 us
    all_to_all x1, blocking collectives, body(): lax.all_to_all(narrow_s.reshape(groups, EXP_DEV * most_rows, cotangent.sh...  20.6 us
    dot_general x1, matrix products, body(): lax.dot_general(moved_h[:, 0], moved_s[:, 0], (((0, 1), (0, 1)), ((), ())...  15.8 us
    psum x1, blocking collectives, body(): expert_load = lax.psum(local_load, ('dp', 'expert'))  14.8 us
    reduce_scatter x1, waiting for transfers between devices, body(): lax.psum_scatter(jnp.stack(products, axis=1), 'dp', scatter_dimension=0,...  7.84 us
    reshape x1, local copies, waits for them, and re-layouts, body(): hidden.reshape(flat_rows, ff_local)  5.71 us
    gather x1, local copies, waits for them, and re-layouts, body(): jnp.take(hidden.reshape(flat_rows, ff_local), source, axis=0)  5.63 us
  transfers between devices with their start and end apart: 2, of which 2 were waited for; matrix products, arithmetic and copies ran while one was open for 8% of the time, Pallas kernels for 0%

commit v1 on v0

--- a/solution.py
+++ b/solution.py
@@ -67,7 +67,12 @@
             tiled=True,
         ),
     )
-    moved_s = lax.all_gather(narrow, "mp", axis=2, tiled=True)
+    ring = [narrow]
+    for hop in range(3):
+        ring.append(lax.ppermute(ring[-1], "mp", [(dev, (dev + 1) % 4) for dev in range(4)]))
+    moved_s = jnp.roll(
+        jnp.concatenate(ring[::-1], axis=2), (lax.axis_index("mp") + 1) * ring[0].shape[2], axis=2
+    )
     moved_h = moved_h.reshape(groups, EXP_DEV, most_rows, ff_local)
     moved_s = moved_s.reshape(groups, EXP_DEV, most_rows, moved_s.shape[2])
     products = [

time: 188 us -> 195 us (1.037)
  blocking collectives: 85.2 us -> 35.9 us
  waiting for transfers between devices: 33.3 us -> 66.4 us
  local copies, waits for them, and re-layouts: 31 us -> 45.6 us
  starting transfers between devices: 0.08 us -> 6.45 us
    ppermute x0 -> x3, waiting for transfers between devices: none -> 59.7 us  [body(): lax.ppermute(ring[-1], 'mp', [(dev, (dev + 1) % 4) for dev in range(4)])]
    all_to_all x1 -> x0, blocking collectives: 49.7 us -> none  [body(): lax.all_to_all(packed_h, 'expert', split_axis=0, concat_axis=0, tiled=True)]
    all_gather x1 -> x0, waiting for transfers between devices: 25.4 us -> none  [body(): moved_s = lax.all_gather(narrow, 'mp', axis=2, tiled=True)]
    unnamed x5 -> x12, local copies, waits for them, and re-layouts: 1.48 us -> 13.6 us
    all_to_all x0 -> x1, starting transfers between devices: none -> 4.83 us  [body(): lax.all_to_all(packed_h, 'expert', split_axis=0, concat_axis=0, tiled=True)]
    concatenate x0 -> x1, local copies, waits for them, and re-layouts: none -> 2.52 us  [body(): jnp.roll(jnp.concatenate(ring[::-1], axis=2), (lax.axis_index('mp') + 1)...]
    select_n x2, other arithmetic: 2.61 us -> 4.61 us  [body(): jnp.take(hidden.reshape(flat_rows, ff_local), source, axis=0)]
  transfers between devices with their start and end apart: 2 -> 5, of which waited for: 2 -> 4; matrix products, arithmetic and copies ran while one was open for 8% -> 16% of each run, Pallas kernels for 0% -> 0%
where the time goes in v1:
time: 195 us
  waiting for transfers between devices  66.4 us (34%)
  local copies, waits for them, and re-layouts  45.6 us (23%)
  blocking collectives  35.9 us (18%)
  matrix products  15.8 us (8%)
  between operations  14.2 us (7%)
  other arithmetic  10.2 us (5%)
  starting transfers between devices  6.45 us (3%)
    ppermute x3, waiting for transfers between devices, body(): lax.ppermute(ring[-1], 'mp', [(dev, (dev + 1) % 4) for dev in range(4)])  59.7 us
    all_to_all x1, blocking collectives, body(): lax.all_to_all(narrow_s.reshape(groups, EXP_DEV * most_rows, cotangent.sh...  20.6 us
    dot_general x1, matrix products, body(): lax.dot_general(moved_h[:, 0], moved_s[:, 0], (((0, 1), (0, 1)), ((), ())...  15.8 us
    psum x1, blocking collectives, body(): expert_load = lax.psum(local_load, ('dp', 'expert'))  15.3 us
    unnamed x12, local copies, waits for them, and re-layouts  13.6 us
    reduce_scatter x1, waiting for transfers between devices, body(): lax.psum_scatter(jnp.stack(products, axis=1), 'dp', scatter_dimension=0,...  6.68 us
    reshape x1, local copies, waits for them, and re-layouts, body(): hidden.reshape(flat_rows, ff_local)  5.71 us
    gather x1, local copies, waits for them, and re-layouts, body(): jnp.take(hidden.reshape(flat_rows, ff_local), source, axis=0)  5.63 us
  transfers between devices with their start and end apart: 5, of which 4 were waited for; matrix products, arithmetic and copies ran while one was open for 16% of the time, Pallas kernels for 0%

profile of v1, /device:TPU:0, one launch (start us, length us, event | category | flops | bytes accessed | tf_op | source)
XLA Modules:
  0.0 194.6 jit_solution(9840566931638105291)
XLA Ops:
  7.2 0.8 fusion.7
  8.2 0.7 fusion.15
  8.9 0.7 broadcast_multiply_fusion.1
  9.6 0.8 copy.16
  11.0 1.1 reduce-window.6
  12.7 3.4 %scatter_custom_fusion = s32[1152]{0:T(1024)S(1)} fusion(s32[768]{0:T(1024)S(1)} %fusion.12, s32[768]{0:T(1024)S(1)} %iota.36, s32[]{:T(128)} %constant.109.clone.1), kind=kCustom, calls=%fused_computation.48 | custom fusion | bytes 4612 | tf_op jit(solution)/shard_map/scatter | solution.py:49
  16.2 0.7 fusion.14
  17.1 0.7 broadcast_reduce_fusion.1
  18.0 0.7 broadcast_multiply_fusion
  19.1 3.4 %scatter_custom_fusion.1 = f32[1152]{0:T(1024)S(1)} fusion(s32[768]{0:T(1024)S(1)} %fusion.12, f32[768]{0:T(1024)S(1)} %broadcast.246, f32[]{:T(128)} %constant.119.clone.1), kind=kCustom, calls=%fused_computation.46 | custom fusion | bytes 4612 | tf_op jit(solution)/shard_map/scatter | solution.py:51
  22.5 4.6 %gather_fusion.1 = f32[1152]{0:T(1024)S(1)} fusion(f32[768]{0:T(1024)S(1)} %reshape.294, s32[2048]{0:T(1024)S(1)} %get-tuple-element.9), kind=kCustom, calls=%fused_computation.1 | custom fusion | bytes 13824 | tf_op jit(solution)/shard_map/jit(_take)/gather | solution.py:53
  27.1 4.2 %gather_fusion.2 = bf16[1152,512]{1,0:T(8,128)(2,1)S(1)} fusion(bf16[384,512]{1,0:T(8,128)(2,1)S(1)} %copy-done, s32[2048]{0:T(1024)S(1)} %get-tuple-element.8), kind=kCustom, calls=%fused_computation.2 | custom fusion | bytes 2363904 | tf_op jit(solution)/shard_map/jit(_take)/gather | solution.py:58
  31.8 20.6 %all_to_all.10 = bf16[4,288,512]{2,1,0:T(8,128)(2,1)} all-to-all(bf16[4,288,512]{2,1,0:T(8,128)(2,1)S(1)} %multiply_convert_fusion), channel_id=1, replica_groups=mesh['dp'=2,'expert'=4,'mp'=4] {'expert'}, dimensions={0} | all-to-all | bytes 2359296 | tf_op jit(solution)/shard_map/all_to_all | solution.py:62
  52.4 1.6 collective-permute-start
  54.1 5.7 %reshape.293 = bf16[768,1792]{1,0:T(8,128)(2,1)S(1)} reshape(bf16[384,2,1792]{2,1,0:T(2,128)(2,1)} %param.7) | data formatting | bytes 5505024 | tf_op jit(solution)/shard_map/reshape | solution.py:54
  59.8 5.6 %gather_fusion = bf16[1152,1792]{1,0:T(8,128)(2,1)} fusion(bf16[768,1792]{1,0:T(8,128)(2,1)S(1)} %reshape.293, s32[2048]{0:T(1024)S(1)} %get-tuple-element.9), kind=kCustom, calls=%fused_computation | custom fusion | bytes 8262144 | tf_op jit(solution)/shard_map/jit(_take)/gather | solution.py:54
  65.4 15.4 %collective-permute-done = bf16[4,288,512]{2,1,0:T(8,128)(2,1)} collective-permute-done((bf16[4,288,512]{2,1,0:T(8,128)(2,1)}, bf16[4,288,512]{2,1,0:T(8,128)(2,1)}, u32[]{:S(2)}, u32[]{:S(2)}) %collective-permute-start) | collective-permute-done | bytes 1179680 | tf_op jit(solution)/shard_map/ppermute | solution.py:72
  80.8 4.6 %broadcast_select_fusion = bf16[4,288,1792]{2,1,0:T(8,128)(2,1)} fusion(bf16[4,288,1792]{2,1,0:T(8,128)(2,1)} %bitcast.38, pred[4,288]{1,0:T(4,128)(4,1)S(1)} %broadcast_in_dim.106), kind=kLoop, calls=%fused_computation.7 | loop fusion | flops 2064384 | bytes 8258688 | tf_op jit(solution)/shard_map/jit(_take)/select_n | solution.py:54
  85.4 4.8 %all-to-all-start = ((bf16[4,288,1792]{2,1,0:T(8,128)(2,1)}), bf16[4,288,1792]{2,1,0:T(8,128)(2,1)}, u32[]{:S(2)}, u32[]{:S(2)}) async-start(bf16[4,288,1792]{2,1,0:T(8,128)(2,1)} %broadcast_select_fusion), calls=%async_computation | async-start | bytes 8257536 | tf_op jit(solution)/shard_map/all_to_all | solution.py:61
  90.3 17.9 %collective-permute-done.1 = bf16[4,288,512]{2,1,0:T(8,128)(2,1)S(1)} collective-permute-done((bf16[4,288,512]{2,1,0:T(8,128)(2,1)}, bf16[4,288,512]{2,1,0:T(8,128)(2,1)S(1)}, u32[]{:S(2)}, u32[]{:S(2)}) %collective-permute-start.1) | collective-permute-done | bytes 1179680 | tf_op jit(solution)/shard_map/ppermute | solution.py:72
  108.2 26.4 %collective-permute-done.2 = bf16[4,288,512]{2,1,0:T(8,128)(2,1)S(1)} collective-permute-done((bf16[4,288,512]{2,1,0:T(8,128)(2,1)S(1)}, bf16[4,288,512]{2,1,0:T(8,128)(2,1)S(1)}, u32[]{:S(2)}, u32[]{:S(2)}) %collective-permute-start.2) | collective-permute-done | bytes 1179680 | tf_op jit(solution)/shard_map/ppermute | solution.py:72
  134.6 1.2 constant_dynamic-update-slice_fusion.7
  135.8 1.2 constant_dynamic-update-slice_fusion.6
  137.0 2.5 %constant_dynamic-update-slice_fusion.5 = bf16[4,288,4096]{2,1,0:T(8,128)(2,1)} fusion(bf16[4,288,4096]{2,1,0:T(8,128)(2,1)} %constant_dynamic-update-slice_fusion.6, bf16[4,288,512]{2,1,0:T(8,128)(2,1)} %collective-permute-done), kind=kLoop, calls=%fused_computation.18 | loop fusion | bytes 2359296
  139.5 2.5 %constant_dynamic-update-slice_fusion.4 = bf16[4,288,4096]{2,1,0:T(8,128)(2,1)} fusion(bf16[4,288,4096]{2,1,0:T(8,128)(2,1)} %constant_dynamic-update-slice_fusion.5, bf16[4,288,512]{2,1,0:T(8,128)(2,1)} %all_to_all.10), kind=kLoop, calls=%fused_computation.17 | loop fusion | bytes 2359296
  141.9 1.2 constant_dynamic-update-slice_fusion.3
  143.1 1.2 constant_dynamic-update-slice_fusion.2
  144.3 2.4 %constant_dynamic-update-slice_fusion.1 = bf16[4,288,4096]{2,1,0:T(8,128)(2,1)} fusion(bf16[4,288,4096]{2,1,0:T(8,128)(2,1)} %constant_dynamic-update-slice_fusion.2, bf16[4,288,512]{2,1,0:T(8,128)(2,1)} %collective-permute-done), kind=kLoop, calls=%fused_computation.14 | loop fusion | bytes 2359296
  146.7 2.5 %constant_dynamic-update-slice_fusion = bf16[4,288,4096]{2,1,0:T(8,128)(2,1)} fusion(bf16[4,288,4096]{2,1,0:T(8,128)(2,1)} %constant_dynamic-update-slice_fusion.1, bf16[4,288,512]{2,1,0:T(8,128)(2,1)} %all_to_all.10), kind=kLoop, calls=%fused_computation.13 | loop fusion | bytes 2359296 | tf_op jit(solution)/shard_map/jit(_roll_dynamic)/concatenate | solution.py:73
  149.2 15.8 %convolution_bitcast_fusion = f32[1792,1,2048]{2,0,1:T(8,128)} fusion(bf16[4,288,1792]{2,1,0:T(8,128)(2,1)} %all-to-all-done, bf16[4,288,4096]{2,1,0:T(8,128)(2,1)} %constant_dynamic-update-slice_fusion, s32[]{:T(128)S(6)} %select_n.126), kind=kOutput, calls=%fused_computation.5 | convolution fusion | flops 8455716864 | bytes 23527428 | tf_op jit(solution)/shard_map/dot_general | solution.py:79
  165.8 15.3 %psum.7 = f32[4]{0:T(128)} all-reduce(f32[4]{0:T(128)S(1)} %select_reduce_fusion), channel_id=1, replica_groups=mesh['dp'=2,'expert'=4,'mp'=4] {'dp','expert'}, use_global_device_ids=true, to_apply=%region_9.10 | all-reduce | flops 4 | bytes 32 | tf_op jit(solution)/shard_map/psum | solution.py:88
  181.1 6.7 %reduce-scatter.2.cloned.1.call-done = f32[896,1,2048]{2,0,1:T(8,128)} async-done(((f32[1792,1,2048]{2,0,1:T(8,128)}), f32[896,1,2048]{2,0,1:T(8,128)}) %reduce-scatter.2.cloned.1.call-update) | async-done | bytes 7340048 | tf_op jit(solution)/shard_map/reduce_scatter | solution.py:86
  (42 shorter events, 3.5 us)
Async XLA Ops:
  7.2 20.0 %copy-start = (bf16[384,512]{1,0:T(8,128)(2,1)S(1)}, bf16[384,512]{1,0:T(8,128)(2,1)}, u32[]{:S(2)}) copy-start(bf16[384,512]{1,0:T(8,128)(2,1)} %param.8) | copy-start | bytes 1179652
  52.4 28.4 %collective-permute-start = (bf16[4,288,512]{2,1,0:T(8,128)(2,1)}, bf16[4,288,512]{2,1,0:T(8,128)(2,1)}, u32[]{:S(2)}, u32[]{:S(2)}) collective-permute-start(bf16[4,288,512]{2,1,0:T(8,128)(2,1)} %all_to_all.10), channel_id=1, source_target_pairs={{0,1},{1,2},{2,3},{3,0},{4,5},{5,6},{6,7},{7,4},{8,9},{9,10},{10,1... | collective-permute-start | bytes 3538952 | tf_op jit(solution)/shard_map/ppermute | solution.py:72
  80.8 27.4 %collective-permute-start.1 = (bf16[4,288,512]{2,1,0:T(8,128)(2,1)}, bf16[4,288,512]{2,1,0:T(8,128)(2,1)S(1)}, u32[]{:S(2)}, u32[]{:S(2)}) collective-permute-start(bf16[4,288,512]{2,1,0:T(8,128)(2,1)} %collective-permute-done), channel_id=1, source_target_pairs={{0,1},{1,2},{2,3},{3,0},{4,5},{5,6},{6,7},{7,4},{8,9},{9,10},{10,1... | collective-permute-start | bytes 3538952 | tf_op jit(solution)/shard_map/ppermute | solution.py:72
  85.4 63.8 %all-to-all-start = ((bf16[4,288,1792]{2,1,0:T(8,128)(2,1)}), bf16[4,288,1792]{2,1,0:T(8,128)(2,1)}, u32[]{:S(2)}, u32[]{:S(2)}) async-start(bf16[4,288,1792]{2,1,0:T(8,128)(2,1)} %broadcast_select_fusion), calls=%async_computation | async-start | bytes 8257536 | tf_op jit(solution)/shard_map/all_to_all | solution.py:61
  90.2 97.5 %reduce-scatter.2.cloned.1.call-start = ((), (), s32[]{:S(2)}) async-start(), calls=%async_computation.3 | async-start | bytes 22020096 | tf_op jit(solution)/shard_map/reduce_scatter | solution.py:86
  108.2 26.4 %collective-permute-start.2 = (bf16[4,288,512]{2,1,0:T(8,128)(2,1)S(1)}, bf16[4,288,512]{2,1,0:T(8,128)(2,1)S(1)}, u32[]{:S(2)}, u32[]{:S(2)}) collective-permute-start(bf16[4,288,512]{2,1,0:T(8,128)(2,1)S(1)} %collective-permute-done.1), channel_id=1, source_target_pairs={{0,1},{1,2},{2,3},{3,0},{4,5},{5,6},{6,7},{7,4},{8,9},{9,10},{10,1... | collective-permute-start | bytes 3538952 | tf_op jit(solution)/shard_map/ppermute | solution.py:72
  165.0 0.7 copy-start.1
Sparse Core Ops, SparseCore 0:
  165.2 22.5 reduce-scatter.1
